TPU v7x, 256 devices: a whole 4x4x8 slice. The times are simulated.
256 devices in a mesh: dp: 8 (over x, y_lo), expert: 16 (over z, core), tensor: 2 (over y_hi).
Axes of the slice: x: 4, y: 4 (y_hi: 2, y_lo: 2; y = y_hi * 2 + y_lo), z: 8, core: 2. Of those that a mesh axis runs over, the one named last changes fastest.
Arguments:
- tokens: bfloat16 [1536, 256, 1280], P(('dp', 'expert', 'tensor')), may hold values from -16 to 16
- cotangent: bfloat16 [1536, 256, 1280], P(('dp', 'expert', 'tensor')), may hold values from -6 to 6
- norm_gain: float32 [1280], replicated, may hold values from 0.5 to 1.5
- slot_keys: bfloat16 [1280, 32], replicated, may hold values from -2 to 2
- w_in: bfloat16 [16, 1280, 2560], P('expert', None, 'tensor'), may hold values from -0.15625 to 0.15625
- w_out: bfloat16 [16, 2560, 1280], P('expert', 'tensor'), may hold values from -0.125 to 0.125
Outputs:
- grad_tokens: bfloat16 [1536, 256, 1280], P(('dp', 'expert', 'tensor'))
- grad_gain: float32 [1280], replicated
- grad_keys: float32 [1280, 32], replicated
- grad_in: bfloat16 [16, 1280, 2560], P('expert', 'dp', 'tensor')
- grad_out: bfloat16 [16, 2560, 1280], P('expert', 'tensor', 'dp')
All inputs are finite; a program needn't handle non-finite values.
Results may differ from a plain program's by a relative error of at most 0.014.
The roundings to bfloat16 on the way count: a program that leaves them out, or rounds other values in their place, can miss the bound.
Values may be sent and summed in bfloat16 or wider, within the bound.
No kernel may reach another device: no remote copies, remote signals or barrier semaphores. Data moves between devices by JAX's collectives and lax.ppermute only.
A program may use at most 128 MiB of HBM per device.

v0:
```python
import jax
import jax.numpy as jnp
from jax import lax
from jax.sharding import PartitionSpec as P

SLOT_PER = 2
EPSILON = 1e-06
ROWS = 24
LANES = 128


def from_everyone(shard, axis):
    devices = lax.axis_size(axis)
    return lax.all_to_all(
        jnp.broadcast_to(shard[None], (devices, *shard.shape)), axis, 0, 0, tiled=True
    )


def swapped(value):
    return lax.ppermute(value, "tensor", [(0, 1), (1, 0)])


def mixing_forward(tokens, gain, slot_keys):
    average = jnp.mean(tokens, axis=-1, keepdims=True, dtype=jnp.float32)
    centred = tokens.astype(jnp.float32) - average
    spread = jnp.mean(centred * centred, axis=-1, keepdims=True)
    inverse = lax.rsqrt(spread + EPSILON)
    scaled = centred * inverse
    normed = (scaled * gain).astype(jnp.bfloat16)
    logits = jnp.einsum("bmd,dn->bmn", normed, slot_keys, preferred_element_type=jnp.float32)
    dispatch = jax.nn.softmax(logits, axis=1)
    combine = jax.nn.softmax(logits, axis=2)
    dispatch_low = dispatch.astype(jnp.bfloat16)
    slot_values = jnp.einsum(
        "bmn,bmd->bnd", dispatch_low, normed, preferred_element_type=jnp.float32
    )
    return (slot_values, combine, (scaled, inverse, normed, dispatch, combine, dispatch_low))


def split_wide(value):
    high = value.astype(jnp.bfloat16)
    low = (value - high.astype(jnp.float32)).astype(jnp.bfloat16)
    return (high, low)


def contract_rows(left, right):
    return lax.dot_general(
        left, right, (((0,), (0,)), ((), ())), preferred_element_type=jnp.float32
    )


def contract_cols(left, right):
    return lax.dot_general(
        left, right, (((1,), (1,)), ((), ())), preferred_element_type=jnp.float32
    )


def summed_everywhere(keys_term, gain_part):
    slots, features = keys_term.shape
    blocks = features // LANES
    group = lax.axis_size("expert")
    flat = jnp.concatenate(
        [
            keys_term.reshape(slots, blocks, LANES).transpose(1, 0, 2).reshape(-1, LANES),
            gain_part.reshape(blocks, LANES),
            jnp.zeros((group * ROWS - (slots + 1) * blocks, LANES), jnp.float32),
        ]
    ).reshape(group, ROWS, LANES)
    mine = jnp.sum(lax.all_to_all(flat, "expert", 0, 0, tiled=True), axis=0)
    mine = jnp.sum(from_everyone(mine, ("dp", "tensor")), axis=0)
    whole = from_everyone(mine, "expert").reshape(-1, LANES)
    keys_sum = whole[: slots * blocks].reshape(blocks, slots, LANES).transpose(1, 0, 2)
    return (keys_sum.reshape(slots, features), whole[slots * blocks :][:blocks].reshape(-1))


def local(tokens, cotangent, norm_gain, slot_keys, w_in, w_out):
    local_imgs, token_count, features = tokens.shape
    slot_count = slot_keys.shape[1]
    experts = slot_count // SLOT_PER
    slot_values, combine, saved = mixing_forward(tokens, norm_gain, slot_keys)
    slot_low = slot_values.astype(jnp.bfloat16)
    slot_inputs = slot_low.reshape(local_imgs, experts, SLOT_PER, features)
    arrived = lax.all_to_all(slot_inputs, "expert", split_axis=1, concat_axis=0, tiled=True)
    own = arrived.reshape(-1, features)
    half = own.shape[0]
    slot_rows = jnp.concatenate([own, swapped(own)])
    combine_low = combine.astype(jnp.bfloat16)
    grad_slots = jnp.einsum(
        "bmn,bmd->bnd", combine_low, cotangent, preferred_element_type=jnp.float32
    )
    grad_slots = grad_slots.astype(jnp.bfloat16).reshape(local_imgs, experts, SLOT_PER, features)
    grads_sent = lax.all_to_all(grad_slots, "expert", split_axis=1, concat_axis=0, tiled=True)
    own_grads = grads_sent.reshape(-1, features)
    grad_rows = jnp.concatenate([own_grads, swapped(own_grads)])
    first_proj = w_in[0]
    second_proj = w_out[0]
    pre_act = jnp.dot(slot_rows, first_proj, preferred_element_type=jnp.float32)
    hidden = jax.nn.gelu(pre_act).astype(jnp.bfloat16)

    def reduced_and_returned(partial):
        theirs = swapped(partial[half:].astype(jnp.bfloat16))
        total = (partial[:half] + theirs.astype(jnp.float32)).astype(jnp.bfloat16)
        return lax.all_to_all(
            total.reshape(arrived.shape), "expert", split_axis=0, concat_axis=1, tiled=True
        ).reshape(local_imgs, slot_count, features)

    returned = reduced_and_returned(
        jnp.dot(hidden, second_proj, preferred_element_type=jnp.float32)
    )
    grad_hidden = contract_cols(grad_rows, second_proj)
    grad_pre = jax.vjp(jax.nn.gelu, pre_act)[1](grad_hidden)[0].astype(jnp.bfloat16)
    grad_back = reduced_and_returned(contract_cols(grad_pre, first_proj))
    second_part = contract_rows(grad_rows, hidden).astype(jnp.bfloat16)
    first_part = contract_rows(slot_rows, grad_pre).astype(jnp.bfloat16)
    grad_second = lax.psum_scatter(second_part, "dp", scatter_dimension=0, tiled=True)
    grad_first = lax.psum_scatter(first_part, "dp", scatter_dimension=0, tiled=True)
    returned, grad_back, second_part, first_part = lax.optimization_barrier(
        (returned, grad_back, second_part, first_part)
    )
    scaled, inverse, normed, dispatch, combine, dispatch_low = saved
    combine_grad = jnp.einsum(
        "bmd,bnd->bmn", cotangent, returned, preferred_element_type=jnp.float32
    )
    grad_dispatch = jnp.einsum(
        "bnd,bmd->bmn", grad_back, normed, preferred_element_type=jnp.float32
    )
    grad_logits = dispatch * (
        grad_dispatch - jnp.sum(dispatch * grad_dispatch, axis=1, keepdims=True)
    )
    grad_logits = grad_logits + combine * (
        combine_grad - jnp.sum(combine * combine_grad, axis=2, keepdims=True)
    )
    high, low = split_wide(grad_logits)
    pair = jnp.concatenate([high, low], axis=2)
    keys_pair = jnp.einsum("bmn,bmd->nd", pair, normed, preferred_element_type=jnp.float32)
    keys_term = keys_pair[:slot_count] + keys_pair[slot_count:]
    gain_part = jnp.sum(grad_back.astype(jnp.float32) * slot_low.astype(jnp.float32), axis=(0, 1))
    keys_sum, gain_sum = summed_everywhere(keys_term, gain_part)
    keys_wide = slot_keys.astype(jnp.float32)
    grad_keys = keys_sum.T
    grad_gain = (gain_sum + jnp.sum(keys_wide * grad_keys, axis=1)) / norm_gain
    weights = jnp.concatenate([dispatch_low, pair], axis=2)
    keys_rows = jnp.broadcast_to(slot_keys.T[None], (local_imgs, slot_count, features))
    values = jnp.concatenate([grad_back, keys_rows, keys_rows], axis=1)
    grad_normed = jnp.einsum("bmn,bnd->bmd", weights, values, preferred_element_type=jnp.float32)
    grad_scaled = grad_normed * norm_gain
    first_mean = jnp.mean(grad_scaled, axis=-1, keepdims=True)
    second_mean = jnp.mean(grad_scaled * scaled, axis=-1, keepdims=True)
    grad_tok = inverse * (grad_scaled - first_mean - scaled * second_mean)
    grad_tokens = (cotangent.astype(jnp.float32) + grad_tok).astype(jnp.bfloat16)
    return (grad_tokens, grad_gain, grad_keys, grad_first[None], grad_second.T[None])


def solution(mesh):
    placed = (
        P(("dp", "expert", "tensor"), None, None),
        P(("dp", "expert", "tensor"), None, None),
        P(),
        P(),
        P("expert", None, "tensor"),
        P("expert", "tensor", None),
    )
    return jax.shard_map(
        local,
        mesh=mesh,
        in_specs=placed,
        out_specs=(
            P(("dp", "expert", "tensor"), None, None),
            P(),
            P(),
            P("expert", "dp", "tensor"),
            P("expert", "tensor", "dp"),
        ),
        check_vma=False,
    )
```

profile of v0, /device:TPU:11, one launch (start us, length us, event | category | flops | bytes accessed | tf_op | source)
XLA Modules:
  0.0 266.0 jit_solution(17931824056655264525)
XLA Ops:
  7.2 2.8 %convert_reduce_fusion = f32[6,256]{1,0:T(8,128)S(1)} fusion(bf16[6,256,1280]{2,1,0:T(8,128)(2,1)} %param.6), kind=kLoop, calls=%fused_computation.5 | loop fusion | flops 3930624 | bytes 3938304 | tf_op jit(solution)/shard_map/reduce_sum | solution.py:24
  11.8 1.7 fusion.61
  16.0 2.4 convolution_convert_fusion.3
  18.4 2.0 reshape.92
  20.4 2.2 copy.26
  22.6 9.2 %all-to-all-start = ((bf16[6,16,2,1280]{3,2,0,1:T(2,128)(2,1)}), bf16[6,16,2,1280]{3,2,0,1:T(2,128)(2,1)}, u32[]{:S(2)}, u32[]{:S(2)}) async-start(bf16[6,16,2,1280]{3,2,0,1:T(2,128)(2,1)} %copy.26), calls=%async_computation | async-start | bytes 983040 | tf_op jit(solution)/shard_map/all_to_all | solution.py:83
  32.5 3.6 %convolution_convert_fusion.2 = bf16[6,32,1280]{2,1,0:T(8,128)(2,1)} fusion(bf16[6,256,1280]{2,1,0:T(8,128)(2,1)} %param.7, f32[6,256]{1,0:T(8,128)S(1)} %get-tuple-element.17, f32[6,256,32]{1,2,0:T(8,128)S(1)} %fusion.61), kind=kOutput, calls=%fused_computation.31 | convolution fusion | flops 126223904 | bytes 4626432 | tf_op jit(solution)/shard_map/bmn,bmd->bnd/dot_general | solution.py:88
  36.0 2.0 reshape.96
  38.0 2.2 copy.29
  40.2 8.2 %all-to-all-done = bf16[6,16,2,1280]{3,2,0,1:T(2,128)(2,1)} async-done(((bf16[6,16,2,1280]{3,2,0,1:T(2,128)(2,1)}), bf16[6,16,2,1280]{3,2,0,1:T(2,128)(2,1)}, u32[]{:S(2)}, u32[]{:S(2)}) %all-to-all-start) | async-done | bytes 491552 | tf_op jit(solution)/shard_map/all_to_all | solution.py:83
  48.4 4.1 %all-to-all-start.2 = ((bf16[6,16,2,1280]{3,2,0,1:T(2,128)(2,1)}), bf16[6,16,2,1280]{3,2,0,1:T(2,128)(2,1)}, u32[]{:S(2)}, u32[]{:S(2)}) async-start(bf16[6,16,2,1280]{3,2,0,1:T(2,128)(2,1)} %copy.29), calls=%async_computation.2 | async-start | bytes 983040 | tf_op jit(solution)/shard_map/all_to_all | solution.py:92
  52.5 2.0 reshape.93
  54.5 2.0 collective-permute-start
  56.5 11.5 %all-to-all-done.2 = bf16[6,16,2,1280]{3,2,0,1:T(2,128)(2,1)} async-done(((bf16[6,16,2,1280]{3,2,0,1:T(2,128)(2,1)}), bf16[6,16,2,1280]{3,2,0,1:T(2,128)(2,1)}, u32[]{:S(2)}, u32[]{:S(2)}) %all-to-all-start.2) | async-done | bytes 491552 | tf_op jit(solution)/shard_map/all_to_all | solution.py:92
  68.0 2.0 reshape.97
  70.0 2.0 collective-permute-start.2
  75.3 1.4 fusion.22
  76.7 7.4 %collective-permute-done.2 = bf16[192,1280]{1,0:T(8,128)(2,1)S(1)} collective-permute-done((bf16[192,1280]{1,0:T(8,128)(2,1)}, bf16[192,1280]{1,0:T(8,128)(2,1)S(1)}, u32[]{:S(2)}, u32[]{:S(2)}) %collective-permute-start.2) | collective-permute-done | bytes 491552 | tf_op jit(solution)/shard_map/ppermute | solution.py:20
  84.1 2.1 fusion.30
  87.2 3.7 %convolution_convert_fusion = bf16[1280,1280]{1,0:T(8,128)(2,1)} fusion(bf16[384,1280]{1,0:T(8,128)(2,1)S(1)} %constant_dynamic-update-slice_fusion, bf16[384,1280]{1,0:T(8,128)(2,1)S(1)} %fusion.30), kind=kOutput, calls=%fused_computation.18 | convolution fusion | flops 1259929600 | bytes 5242880 | tf_op jit(solution)/shard_map/dot_general | solution.py:47
  91.0 2.8 %fusion.20 = f32[384,1280]{1,0:T(8,128)S(1)} fusion(bf16[384,1280]{1,0:T(8,128)(2,1)} %copy-done.19, bf16[1,1280,1280]{2,1,0:T(8,128)(2,1)S(1)} %copy-done), kind=kOutput, calls=%fused_computation.25 | convolution fusion | flops 1258291200 | bytes 6225920 | tf_op jit(solution)/shard_map/dot_general | solution.py:53
  93.9 2.1 collective-permute-start.3
  96.0 1.8 fusion.18
  100.9 21.8 %collective-permute-done.3 = bf16[192,1280]{1,0:T(8,128)(2,1)S(1)} collective-permute-done((bf16[192,1280]{1,0:T(8,128)(2,1)S(1)}, bf16[192,1280]{1,0:T(8,128)(2,1)S(1)}, u32[]{:S(2)}, u32[]{:S(2)}) %collective-permute-start.3) | collective-permute-done | bytes 491552 | tf_op jit(solution)/shard_map/ppermute | solution.py:20
  123.5 2.0 reshape.98
  125.5 7.6 %all-to-all-start.3 = ((bf16[96,1,2,1280]{3,2,1,0:T(2,128)(2,1)}), bf16[96,1,2,1280]{3,2,1,0:T(2,128)(2,1)}, u32[]{:S(2)}, u32[]{:S(2)}) async-start(bf16[96,1,2,1280]{3,2,1,0:T(2,128)(2,1)} %bitcast.81), calls=%async_computation.3 | async-start | bytes 983040 | tf_op jit(solution)/shard_map/all_to_all | solution.py:103
  133.1 5.7 %convolution_convert_fusion.1 = bf16[1280,1280]{1,0:T(8,128)(2,1)} fusion(bf16[384,1280]{1,0:T(8,128)(2,1)} %copy-done.9, f32[384,1280]{1,0:T(8,128)} %copy-done.17), kind=kOutput, calls=%fused_computation.19 | convolution fusion | flops 1264353280 | bytes 6225920 | tf_op jit(solution)/shard_map/dot_general | solution.py:47
  138.8 15.9 %collective-permute-done.1 = bf16[192,1280]{1,0:T(8,128)(2,1)} collective-permute-done((bf16[192,1280]{1,0:T(8,128)(2,1)}, bf16[192,1280]{1,0:T(8,128)(2,1)}, u32[]{:S(2)}, u32[]{:S(2)}) %collective-permute-start.1) | collective-permute-done | bytes 491552 | tf_op jit(solution)/shard_map/ppermute | solution.py:20
  154.8 2.2 fusion.49
  157.0 2.0 reshape.94
  159.0 8.1 %all-to-all-start.1 = ((bf16[96,1,2,1280]{3,2,1,0:T(2,128)(2,1)}), bf16[96,1,2,1280]{3,2,1,0:T(2,128)(2,1)}, u32[]{:S(2)}, u32[]{:S(2)}) async-start(bf16[96,1,2,1280]{3,2,1,0:T(2,128)(2,1)} %bitcast.82), calls=%async_computation.1 | async-start | bytes 983040 | tf_op jit(solution)/shard_map/all_to_all | solution.py:103
  167.8 2.1 copy.31
  169.9 2.0 reshape.99
  171.9 11.7 %all-to-all-done.1 = bf16[96,1,2,1280]{3,2,1,0:T(2,128)(2,1)} async-done(((bf16[96,1,2,1280]{3,2,1,0:T(2,128)(2,1)}), bf16[96,1,2,1280]{3,2,1,0:T(2,128)(2,1)}, u32[]{:S(2)}, u32[]{:S(2)}) %all-to-all-start.1) | async-done | bytes 491552 | tf_op jit(solution)/shard_map/all_to_all | solution.py:103
  183.6 2.2 copy.28
  185.7 2.0 reshape.95
  187.7 3.6 %convolution_bitcast_fusion.1 = f32[6,256,32]{1,2,0:T(8,128)S(1)} fusion(bf16[6,32,1280]{2,1,0:T(8,128)(2,1)} %reshape.95, bf16[6,256,1280]{2,1,0:T(8,128)(2,1)} %param.7), kind=kOutput, calls=%fused_computation.55 | convolution fusion | flops 125829120 | bytes 4620288 | tf_op jit(solution)/shard_map/bmd,bnd->bmn/dot_general | solution.py:121
  191.8 1.5 fusion.69
  194.2 1.6 convolution_bitcast_fusion
  198.8 1.5 maximum_maximum_fusion
  200.3 3.4 %all-to-all-start.4 = ((f32[16,24,128]{2,1,0:T(8,128)}), f32[16,24,128]{2,1,0:T(8,128)S(1)}, u32[]{:S(2)}, u32[]{:S(2)}) async-start(f32[16,24,128]{2,1,0:T(8,128)} %bitcast.84), calls=%async_computation.4 | async-start | bytes 393216 | tf_op jit(solution)/shard_map/all_to_all | solution.py:69
  204.7 7.8 %multiply_reduce_fusion = (f32[6,256]{1,0:T(8,128)S(1)}, f32[6,256]{1,0:T(8,128)S(1)}, f32[6,256,1280]{2,1,0:T(8,128)}) fusion(f32[1280]{0:T(1024)} %param.8, f32[6,256]{1,0:T(8,128)S(1)} %add_rsqrt_fusion, f32[6,256]{1,0:T(8,128)S(1)} %broadcast_multiply_fusion.2, bf16[6,256,1280]{2,1,0:T(8,128)(2,1)} %param.6, ...), kind=kOutput, calls=%fused_computation.20 | convolution fusion | flops 396555264 | bytes 13104128 | tf_op jit(solution)/shard_map/bmn,bnd->bmd/dot_general | solution.py:145
  214.3 9.5 %all-to-all-start.5 = ((f32[16,24,128]{2,1,0:T(8,128)}), f32[16,24,128]{2,1,0:T(8,128)S(1)}, u32[]{:S(2)}, u32[]{:S(2)}) async-start(f32[16,24,128]{2,1,0:T(8,128)} %broadcast_in_dim.14), calls=%async_computation.5 | async-start | bytes 393216 | tf_op jit(solution)/shard_map/all_to_all | solution.py:14
  224.5 7.5 %all-to-all-done.5 = f32[16,24,128]{2,1,0:T(8,128)S(1)} async-done(((f32[16,24,128]{2,1,0:T(8,128)}), f32[16,24,128]{2,1,0:T(8,128)S(1)}, u32[]{:S(2)}, u32[]{:S(2)}) %all-to-all-start.5) | async-done | bytes 196640 | tf_op jit(solution)/shard_map/all_to_all | solution.py:14
  232.7 5.7 %all-to-all-start.6 = ((f32[16,24,128]{2,1,0:T(8,128)}), f32[16,24,128]{2,1,0:T(8,128)S(1)}, u32[]{:S(2)}, u32[]{:S(2)}) async-start(f32[16,24,128]{2,1,0:T(8,128)} %broadcast_in_dim.15), calls=%async_computation.6 | async-start | bytes 393216 | tf_op jit(solution)/shard_map/all_to_all | solution.py:14
  238.4 8.5 %fusion.14 = bf16[6,256,1280]{2,1,0:T(8,128)(2,1)} fusion(bf16[6,256,1280]{2,1,0:T(8,128)(2,1)} %param.6, bf16[6,256,1280]{2,1,0:T(8,128)(2,1)} %param.7, f32[6,256,1280]{2,1,0:T(8,128)} %get-tuple-element.19, f32[6,256]{1,0:T(8,128)} %get-tuple-element.20, f32[6,256]{1,0:T(8,128)} %get-tuple-element.21, f32[1280]{0:T(1024)} %param.8, ...), kind=kLoop, calls=%fused_computation.16 | loop fusion | flops 21626880 | bytes 19690496 | tf_op jit(solution)/shard_map/convert_element_type | solution.py:150
  246.9 1.7 all-to-all-done.6
  250.6 8.5 %reduce-scatter.5.cloned.1.call-done = bf16[160,1280]{1,0:T(8,128)(2,1)} async-done(((bf16[1280,1280]{1,0:T(8,128)(2,1)}), bf16[160,1280]{1,0:T(8,128)(2,1)}) %reduce-scatter.5.cloned.1.call-update) | async-done | bytes 409616 | tf_op jit(solution)/shard_map/reduce_scatter | solution.py:115
  (83 shorter events, 24.3 us)
Async XLA Ops:
  7.2 68.1 %copy-start = (bf16[1,1280,1280]{2,1,0:T(8,128)(2,1)S(1)}, bf16[1,1280,1280]{2,1,0:T(8,128)(2,1)}, u32[]{:S(2)}) copy-start(bf16[1,1280,1280]{2,1,0:T(8,128)(2,1)} %param.10) | copy-start | bytes 9830404
  7.2 3.4 %copy-start.1 = (bf16[6,256,1280]{2,1,0:T(8,128)(2,1)S(1)}, bf16[6,256,1280]{2,1,0:T(8,128)(2,1)}, u32[]{:S(2)}) copy-start(bf16[6,256,1280]{2,1,0:T(8,128)(2,1)} %param.6) | copy-start | bytes 11796484
  7.2 4.6 %copy-start.14 = (f32[1280]{0:T(1024)S(1)}, f32[1280]{0:T(1024)}, u32[]{:S(2)}) copy-start(f32[1280]{0:T(1024)} %param.8) | copy-start | bytes 15364
  7.2 4.6 %copy-start.7 = (bf16[1280,32]{0,1:T(8,128)(2,1)S(1)}, bf16[1280,32]{0,1:T(8,128)(2,1)}, u32[]{:S(2)}) copy-start(bf16[1280,32]{0,1:T(8,128)(2,1)} %param.9) | copy-start | bytes 245764
  10.6 194.0 %copy-start.12 = (f32[6,256]{1,0:T(8,128)}, f32[6,256]{1,0:T(8,128)S(1)}, u32[]{:S(2)}) copy-start(f32[6,256]{1,0:T(8,128)S(1)} %broadcast_multiply_fusion.2) | copy-start | bytes 18436
  11.8 192.8 %copy-start.13 = (f32[6,256]{1,0:T(8,128)}, f32[6,256]{1,0:T(8,128)S(1)}, u32[]{:S(2)}) copy-start(f32[6,256]{1,0:T(8,128)S(1)} %add_rsqrt_fusion) | copy-start | bytes 18436
  14.6 0.7 copy-start.5
  15.4 0.6 copy-start.11
  22.6 25.8 %all-to-all-start = ((bf16[6,16,2,1280]{3,2,0,1:T(2,128)(2,1)}), bf16[6,16,2,1280]{3,2,0,1:T(2,128)(2,1)}, u32[]{:S(2)}, u32[]{:S(2)}) async-start(bf16[6,16,2,1280]{3,2,0,1:T(2,128)(2,1)} %copy.26), calls=%async_computation | async-start | bytes 983040 | tf_op jit(solution)/shard_map/all_to_all | solution.py:83
  48.4 19.7 %all-to-all-start.2 = ((bf16[6,16,2,1280]{3,2,0,1:T(2,128)(2,1)}), bf16[6,16,2,1280]{3,2,0,1:T(2,128)(2,1)}, u32[]{:S(2)}, u32[]{:S(2)}) async-start(bf16[6,16,2,1280]{3,2,0,1:T(2,128)(2,1)} %copy.29), calls=%async_computation.2 | async-start | bytes 983040 | tf_op jit(solution)/shard_map/all_to_all | solution.py:92
  52.5 198.1 %reduce-scatter.3.cloned.1.call-start = ((), (), s32[]{:S(2)}) async-start(), calls=%async_computation.9 | async-start | bytes 3686400 | tf_op jit(solution)/shard_map/reduce_scatter | solution.py:116
  54.5 19.6 %collective-permute-start = (bf16[192,1280]{1,0:T(8,128)(2,1)}, bf16[192,1280]{1,0:T(8,128)(2,1)}, u32[]{:S(2)}, u32[]{:S(2)}) collective-permute-start(bf16[192,1280]{1,0:T(8,128)(2,1)} %reshape.93), channel_id=1, source_target_pairs={{0,1},{1,0},{2,3},{3,2},{4,5},{5,4},{6,7},{7,6},{8,9},{9,8},{10,11... | collective-permute-start | bytes 1474568 | tf_op jit(solution)/shard_map/ppermute | solution.py:20
  70.0 14.1 %collective-permute-start.2 = (bf16[192,1280]{1,0:T(8,128)(2,1)}, bf16[192,1280]{1,0:T(8,128)(2,1)S(1)}, u32[]{:S(2)}, u32[]{:S(2)}) collective-permute-start(bf16[192,1280]{1,0:T(8,128)(2,1)} %reshape.97), channel_id=1, source_target_pairs={{0,1},{1,0},{2,3},{3,2},{4,5},{5,4},{6,7},{7,6},{8,9},{9,8},{10,11... | collective-permute-start | bytes 1474568 | tf_op jit(solution)/shard_map/ppermute | solution.py:20
  75.3 8.9 %copy-start.15 = (bf16[1,1280,1280]{2,1,0:T(8,128)(2,1)S(1)}, bf16[1,1280,1280]{2,1,0:T(8,128)(2,1)}, u32[]{:S(2)}) copy-start(bf16[1,1280,1280]{2,1,0:T(8,128)(2,1)} %param.11) | copy-start | bytes 9830404
  76.7 9.5 %copy-start.17 = (f32[384,1280]{1,0:T(8,128)}, f32[384,1280]{1,0:T(8,128)S(1)}, u32[]{:S(2)}) copy-start(f32[384,1280]{1,0:T(8,128)S(1)} %fusion.22) | copy-start | bytes 5898244
  84.1 2.1 copy-start.9
  86.3 1.0 copy-start.19
  91.0 5.0 %copy-start.16 = (bf16[1,1280,1280]{2,1,0:T(8,128)(2,1)S(1)}, bf16[1,1280,1280]{2,1,0:T(8,128)(2,1)}, u32[]{:S(2)}) copy-start(bf16[1,1280,1280]{2,1,0:T(8,128)(2,1)} %param.11) | copy-start | bytes 9830404
  91.0 5.0 %copy-start.18 = (f32[384,1280]{1,0:T(8,128)S(1)}, f32[384,1280]{1,0:T(8,128)}, u32[]{:S(2)}) copy-start(f32[384,1280]{1,0:T(8,128)} %copy-done.17) | copy-start | bytes 5898244
  93.9 28.7 %collective-permute-start.3 = (bf16[192,1280]{1,0:T(8,128)(2,1)S(1)}, bf16[192,1280]{1,0:T(8,128)(2,1)S(1)}, u32[]{:S(2)}, u32[]{:S(2)}) collective-permute-start(bf16[192,1280]{1,0:T(8,128)(2,1)S(1)} %slice.59), channel_id=1, source_target_pairs={{0,1},{1,0},{2,3},{3,2},{4,5},{5,4},{6,7},{7,6},{8,9},{9,8},{10,11... | collective-permute-start | bytes 1474568 | tf_op jit(solution)/shard_map/ppermute | solution.py:20
  97.8 1.3 copy-start.4
  99.9 54.9 %collective-permute-start.1 = (bf16[192,1280]{1,0:T(8,128)(2,1)}, bf16[192,1280]{1,0:T(8,128)(2,1)}, u32[]{:S(2)}, u32[]{:S(2)}) collective-permute-start(bf16[192,1280]{1,0:T(8,128)(2,1)} %slice.60), channel_id=1, source_target_pairs={{0,1},{1,0},{2,3},{3,2},{4,5},{5,4},{6,7},{7,6},{8,9},{9,8},{10,11... | collective-permute-start | bytes 1474568 | tf_op jit(solution)/shard_map/ppermute | solution.py:20
  125.5 33.5 %all-to-all-start.3 = ((bf16[96,1,2,1280]{3,2,1,0:T(2,128)(2,1)}), bf16[96,1,2,1280]{3,2,1,0:T(2,128)(2,1)}, u32[]{:S(2)}, u32[]{:S(2)}) async-start(bf16[96,1,2,1280]{3,2,1,0:T(2,128)(2,1)} %bitcast.81), calls=%async_computation.3 | async-start | bytes 983040 | tf_op jit(solution)/shard_map/all_to_all | solution.py:103
  133.1 126.0 %reduce-scatter.5.cloned.1.call-start = ((), (), s32[]{:S(2)}) async-start(), calls=%async_computation.10 | async-start | bytes 3686400 | tf_op jit(solution)/shard_map/reduce_scatter | solution.py:115
  159.0 24.6 %all-to-all-start.1 = ((bf16[96,1,2,1280]{3,2,1,0:T(2,128)(2,1)}), bf16[96,1,2,1280]{3,2,1,0:T(2,128)(2,1)}, u32[]{:S(2)}, u32[]{:S(2)}) async-start(bf16[96,1,2,1280]{3,2,1,0:T(2,128)(2,1)} %bitcast.82), calls=%async_computation.1 | async-start | bytes 983040 | tf_op jit(solution)/shard_map/all_to_all | solution.py:103
  183.6 7.8 %copy-start.10 = (f32[6,256,32]{1,2,0:T(8,128)S(1)}, f32[6,256,32]{1,2,0:T(8,128)}, u32[]{:S(2)}) copy-start(f32[6,256,32]{1,2,0:T(8,128)} %get-tuple-element.18) | copy-start | bytes 589828
  187.7 4.0 %copy-start.2 = (bf16[6,256,1280]{2,1,0:T(8,128)(2,1)S(1)}, bf16[6,256,1280]{2,1,0:T(8,128)(2,1)}, u32[]{:S(2)}) copy-start(bf16[6,256,1280]{2,1,0:T(8,128)(2,1)} %param.6) | copy-start | bytes 11796484
  187.7 4.0 %copy-start.3 = (bf16[6,32,1280]{2,1,0:T(8,128)(2,1)S(1)}, bf16[6,32,1280]{2,1,0:T(8,128)(2,1)}, u32[]{:S(2)}) copy-start(bf16[6,32,1280]{2,1,0:T(8,128)(2,1)} %reshape.99) | copy-start | bytes 1474564
  191.8 1.5 copy-start.6
  194.2 1.6 copy-start.20
  194.2 1.6 copy-start.21
  200.3 13.3 %all-to-all-start.4 = ((f32[16,24,128]{2,1,0:T(8,128)}), f32[16,24,128]{2,1,0:T(8,128)S(1)}, u32[]{:S(2)}, u32[]{:S(2)}) async-start(f32[16,24,128]{2,1,0:T(8,128)} %bitcast.84), calls=%async_computation.4 | async-start | bytes 393216 | tf_op jit(solution)/shard_map/all_to_all | solution.py:69
  214.3 17.6 %all-to-all-start.5 = ((f32[16,24,128]{2,1,0:T(8,128)}), f32[16,24,128]{2,1,0:T(8,128)S(1)}, u32[]{:S(2)}, u32[]{:S(2)}) async-start(f32[16,24,128]{2,1,0:T(8,128)} %broadcast_in_dim.14), calls=%async_computation.5 | async-start | bytes 393216 | tf_op jit(solution)/shard_map/all_to_all | solution.py:14
  232.7 15.9 %all-to-all-start.6 = ((f32[16,24,128]{2,1,0:T(8,128)}), f32[16,24,128]{2,1,0:T(8,128)S(1)}, u32[]{:S(2)}, u32[]{:S(2)}) async-start(f32[16,24,128]{2,1,0:T(8,128)} %broadcast_in_dim.15), calls=%async_computation.6 | async-start | bytes 393216 | tf_op jit(solution)/shard_map/all_to_all | solution.py:14
  238.4 10.2 %copy-start.8 = (bf16[1280,32]{0,1:T(8,128)(2,1)S(1)}, bf16[1280,32]{0,1:T(8,128)(2,1)}, u32[]{:S(2)}) copy-start(bf16[1280,32]{0,1:T(8,128)(2,1)} %param.9) | copy-start | bytes 245764
Sparse Core Ops, SparseCore 0:
  91.1 90.7 reduce-scatter.2
  185.0 74.0 reduce-scatter.4
where the time goes:
time: 268 us; the launch traced here: 266 us
  waiting for transfers between devices  95.2 us (36%)
  starting transfers between devices  54.8 us (20%)
  matrix products  39.8 us (15%)
  local copies, waits for them, and re-layouts  36.9 us (14%)
  other arithmetic  24.8 us (9%)
  between operations  14.5 us (5%)
    ppermute x4, waiting for transfers between devices, swapped(): return lax.ppermute(value, 'tensor', [(0, 1), (1, 0)])  45.1 us
    all_to_all x2, starting transfers between devices, reduced_and_returned(): lax.all_to_all(total.reshape(arrived.shape), 'expert', split_axis=0, conc...  15.7 us
    all_to_all x2, starting transfers between devices, from_everyone(): lax.all_to_all(jnp.broadcast_to(shard[None], (devices, *shard.shape)), ax...  15.2 us
    all_to_all x2, waiting for transfers between devices, reduced_and_returned(): lax.all_to_all(total.reshape(arrived.shape), 'expert', split_axis=0, conc...  11.7 us
    all_to_all x1, waiting for transfers between devices, local(): lax.all_to_all(grad_slots, 'expert', split_axis=1, concat_axis=0, tiled=T...  11.5 us
    dot_general x2, matrix products, contract_rows(): lax.dot_general(left, right, (((0,), (0,)), ((), ())), preferred_element_...  9.39 us
    all_to_all x2, waiting for transfers between devices, from_everyone(): lax.all_to_all(jnp.broadcast_to(shard[None], (devices, *shard.shape)), ax...  9.2 us
    all_to_all x1, starting transfers between devices, local(): lax.all_to_all(slot_inputs, 'expert', split_axis=1, concat_axis=0, tiled=...  9.15 us
  transfers between devices with their start and end apart: 13, of which 10 were waited for; matrix products, arithmetic and copies ran while one was open for 29% of the time, Pallas kernels for 0%

commit v1 on v0

--- a/solution.py
+++ b/solution.py
@@ -80,7 +80,12 @@
     slot_values, combine, saved = mixing_forward(tokens, norm_gain, slot_keys)
     slot_low = slot_values.astype(jnp.bfloat16)
     slot_inputs = slot_low.reshape(local_imgs, experts, SLOT_PER, features)
-    arrived = lax.all_to_all(slot_inputs, "expert", split_axis=1, concat_axis=0, tiled=True)
+    arrived = jnp.concatenate(
+        lax.all_to_all(
+            jnp.stack(jnp.split(slot_inputs, lax.axis_size("expert"), axis=1)), "expert", 0, 0
+        ),
+        axis=0,
+    )
     own = arrived.reshape(-1, features)
     half = own.shape[0]
     slot_rows = jnp.concatenate([own, swapped(own)])

time: 268 us -> 289 us (1.078)
  local copies, waits for them, and re-layouts: 36.9 us -> 56.9 us
    unnamed x46 -> x61, local copies, waits for them, and re-layouts: 6.33 us -> 27.1 us
    another operation x0 -> x2, local copies, waits for them, and re-layouts: none -> 3.38 us  [the longest x1 1.99 us: local(): own = arrived.reshape(-1, features)]
  transfers between devices with their start and end apart: 13 -> 13, of which waited for: 10 -> 10; matrix products, arithmetic and copies ran while one was open for 29% -> 27% of each run, Pallas kernels for 0% -> 0%
where the time goes in v1:
time: 289 us; the launch traced here: 286 us
  waiting for transfers between devices  95.2 us (33%)
  local copies, waits for them, and re-layouts  56.9 us (20%)
  starting transfers between devices  54.8 us (19%)
  matrix products  39.8 us (14%)
  other arithmetic  24.8 us (9%)
  between operations  14.5 us (5%)
    ppermute x4, waiting for transfers between devices, swapped(): return lax.ppermute(value, 'tensor', [(0, 1), (1, 0)])  45.1 us
    unnamed x61, local copies, waits for them, and re-layouts  27.1 us
    all_to_all x2, starting transfers between devices, reduced_and_returned(): lax.all_to_all(total.reshape(arrived.shape), 'expert', split_axis=0, conc...  15.7 us
    all_to_all x2, starting transfers between devices, from_everyone(): lax.all_to_all(jnp.broadcast_to(shard[None], (devices, *shard.shape)), ax...  15.2 us
    all_to_all x2, waiting for transfers between devices, reduced_and_returned(): lax.all_to_all(total.reshape(arrived.shape), 'expert', split_axis=0, conc...  11.7 us
    all_to_all x1, waiting for transfers between devices, local(): lax.all_to_all(grad_slots, 'expert', split_axis=1, concat_axis=0, tiled=T...  11.5 us
    dot_general x2, matrix products, contract_rows(): lax.dot_general(left, right, (((0,), (0,)), ((), ())), preferred_element_...  9.39 us
    all_to_all x2, waiting for transfers between devices, from_everyone(): lax.all_to_all(jnp.broadcast_to(shard[None], (devices, *shard.shape)), ax...  9.2 us
  transfers between devices with their start and end apart: 13, of which 10 were waited for; matrix products, arithmetic and copies ran while one was open for 27% of the time, Pallas kernels for 0%

profile of v1, /device:TPU:11, one launch (start us, length us, event | category | flops | bytes accessed | tf_op | source)
XLA Modules:
  0.0 285.9 jit_solution(12586751814353058134)
XLA Ops:
  7.2 2.8 convert_reduce_fusion
  11.8 1.7 fusion.61
  16.0 2.4 convolution_convert_fusion.3
  18.4 2.0 reshape.88
  37.0 1.4 constant_dynamic-update-slice_fusion.3
  42.5 9.2 %all-to-all-start = ((bf16[16,6,1,2,1280]{4,3,1,2,0:T(2,128)(2,1)}), bf16[16,6,1,2,1280]{4,3,1,2,0:T(2,128)(2,1)}, u32[]{:S(2)}, u32[]{:S(2)}) async-start(bf16[16,6,1,2,1280]{4,3,1,2,0:T(2,128)(2,1)} %constant_dynamic-update-slice_fusion), calls=%async_computation | async-start | bytes 983040 | tf_op jit(solution)/shard_map/all_to_all | solution.py:84
  52.4 3.6 %convolution_convert_fusion.2 = bf16[6,32,1280]{2,1,0:T(8,128)(2,1)} fusion(bf16[6,256,1280]{2,1,0:T(8,128)(2,1)} %param.7, f32[6,256]{1,0:T(8,128)S(1)} %get-tuple-element.17, f32[6,256,32]{1,2,0:T(8,128)S(1)} %fusion.61), kind=kOutput, calls=%fused_computation.31 | convolution fusion | flops 126223904 | bytes 4626432 | tf_op jit(solution)/shard_map/bmn,bmd->bnd/dot_general | solution.py:93
  56.0 2.0 reshape.91
  58.0 2.2 copy.86
  60.2 8.2 %all-to-all-done = bf16[16,6,1,2,1280]{4,3,1,2,0:T(2,128)(2,1)} async-done(((bf16[16,6,1,2,1280]{4,3,1,2,0:T(2,128)(2,1)}), bf16[16,6,1,2,1280]{4,3,1,2,0:T(2,128)(2,1)}, u32[]{:S(2)}, u32[]{:S(2)}) %all-to-all-start) | async-done | bytes 491552 | tf_op jit(solution)/shard_map/all_to_all | solution.py:84
  68.3 4.1 %all-to-all-start.2 = ((bf16[6,16,2,1280]{3,2,0,1:T(2,128)(2,1)}), bf16[6,16,2,1280]{3,2,0,1:T(2,128)(2,1)}, u32[]{:S(2)}, u32[]{:S(2)}) async-start(bf16[6,16,2,1280]{3,2,0,1:T(2,128)(2,1)} %copy.86), calls=%async_computation.2 | async-start | bytes 983040 | tf_op jit(solution)/shard_map/all_to_all | solution.py:97
  72.5 2.0 reshape_reshape.3
  74.5 2.0 collective-permute-start
  76.5 11.5 %all-to-all-done.2 = bf16[6,16,2,1280]{3,2,0,1:T(2,128)(2,1)} async-done(((bf16[6,16,2,1280]{3,2,0,1:T(2,128)(2,1)}), bf16[6,16,2,1280]{3,2,0,1:T(2,128)(2,1)}, u32[]{:S(2)}, u32[]{:S(2)}) %all-to-all-start.2) | async-done | bytes 491552 | tf_op jit(solution)/shard_map/all_to_all | solution.py:97
  88.0 2.0 reshape.92
  90.0 2.0 collective-permute-start.2
  95.2 1.4 fusion.22
  96.7 7.4 %collective-permute-done.2 = bf16[192,1280]{1,0:T(8,128)(2,1)S(1)} collective-permute-done((bf16[192,1280]{1,0:T(8,128)(2,1)}, bf16[192,1280]{1,0:T(8,128)(2,1)S(1)}, u32[]{:S(2)}, u32[]{:S(2)}) %collective-permute-start.2) | collective-permute-done | bytes 491552 | tf_op jit(solution)/shard_map/ppermute | solution.py:20
  104.1 2.1 fusion.30
  107.2 3.7 %convolution_convert_fusion = bf16[1280,1280]{1,0:T(8,128)(2,1)} fusion(bf16[384,1280]{1,0:T(8,128)(2,1)S(1)} %constant_dynamic-update-slice_fusion.16, bf16[384,1280]{1,0:T(8,128)(2,1)S(1)} %fusion.30), kind=kOutput, calls=%fused_computation.18 | convolution fusion | flops 1259929600 | bytes 5242880 | tf_op jit(solution)/shard_map/dot_general | solution.py:47
  111.0 2.8 fusion.20
  113.8 2.1 collective-permute-start.3
  116.0 1.8 fusion.18
  120.8 21.8 %collective-permute-done.3 = bf16[192,1280]{1,0:T(8,128)(2,1)S(1)} collective-permute-done((bf16[192,1280]{1,0:T(8,128)(2,1)S(1)}, bf16[192,1280]{1,0:T(8,128)(2,1)S(1)}, u32[]{:S(2)}, u32[]{:S(2)}) %collective-permute-start.3) | collective-permute-done | bytes 491552 | tf_op jit(solution)/shard_map/ppermute | solution.py:20
  143.5 2.0 reshape.93
  145.5 7.6 %all-to-all-start.3 = ((bf16[96,1,2,1280]{3,2,1,0:T(2,128)(2,1)}), bf16[96,1,2,1280]{3,2,1,0:T(2,128)(2,1)}, u32[]{:S(2)}, u32[]{:S(2)}) async-start(bf16[96,1,2,1280]{3,2,1,0:T(2,128)(2,1)} %bitcast.172), calls=%async_computation.3 | async-start | bytes 983040 | tf_op jit(solution)/shard_map/all_to_all | solution.py:108
  153.1 5.7 %convolution_convert_fusion.1 = bf16[1280,1280]{1,0:T(8,128)(2,1)} fusion(bf16[384,1280]{1,0:T(8,128)(2,1)} %copy-done.9, f32[384,1280]{1,0:T(8,128)} %copy-done.17), kind=kOutput, calls=%fused_computation.19 | convolution fusion | flops 1264353280 | bytes 6225920 | tf_op jit(solution)/shard_map/dot_general | solution.py:47
  158.8 15.9 %collective-permute-done.1 = bf16[192,1280]{1,0:T(8,128)(2,1)} collective-permute-done((bf16[192,1280]{1,0:T(8,128)(2,1)}, bf16[192,1280]{1,0:T(8,128)(2,1)}, u32[]{:S(2)}, u32[]{:S(2)}) %collective-permute-start.1) | collective-permute-done | bytes 491552 | tf_op jit(solution)/shard_map/ppermute | solution.py:20
  174.7 2.2 fusion.49
  176.9 2.0 reshape.89
  178.9 8.1 %all-to-all-start.1 = ((bf16[96,1,2,1280]{3,2,1,0:T(2,128)(2,1)}), bf16[96,1,2,1280]{3,2,1,0:T(2,128)(2,1)}, u32[]{:S(2)}, u32[]{:S(2)}) async-start(bf16[96,1,2,1280]{3,2,1,0:T(2,128)(2,1)} %bitcast.173), calls=%async_computation.1 | async-start | bytes 983040 | tf_op jit(solution)/shard_map/all_to_all | solution.py:108
  187.7 2.1 copy.88
  189.9 2.0 reshape.94
  191.8 11.7 %all-to-all-done.1 = bf16[96,1,2,1280]{3,2,1,0:T(2,128)(2,1)} async-done(((bf16[96,1,2,1280]{3,2,1,0:T(2,128)(2,1)}), bf16[96,1,2,1280]{3,2,1,0:T(2,128)(2,1)}, u32[]{:S(2)}, u32[]{:S(2)}) %all-to-all-start.1) | async-done | bytes 491552 | tf_op jit(solution)/shard_map/all_to_all | solution.py:108
  203.5 2.2 copy.85
  205.7 2.0 reshape.90
  207.7 3.6 %convolution_bitcast_fusion.1 = f32[6,256,32]{1,2,0:T(8,128)S(1)} fusion(bf16[6,32,1280]{2,1,0:T(8,128)(2,1)} %reshape.90, bf16[6,256,1280]{2,1,0:T(8,128)(2,1)} %param.7), kind=kOutput, calls=%fused_computation.55 | convolution fusion | flops 125829120 | bytes 4620288 | tf_op jit(solution)/shard_map/bmd,bnd->bmn/dot_general | solution.py:126
  211.7 1.5 fusion.69
  214.2 1.6 convolution_bitcast_fusion
  218.8 1.5 maximum_maximum_fusion
  220.3 3.4 %all-to-all-start.4 = ((f32[16,24,128]{2,1,0:T(8,128)}), f32[16,24,128]{2,1,0:T(8,128)S(1)}, u32[]{:S(2)}, u32[]{:S(2)}) async-start(f32[16,24,128]{2,1,0:T(8,128)} %bitcast.175), calls=%async_computation.4 | async-start | bytes 393216 | tf_op jit(solution)/shard_map/all_to_all | solution.py:69
  224.6 7.8 %multiply_reduce_fusion = (f32[6,256]{1,0:T(8,128)S(1)}, f32[6,256]{1,0:T(8,128)S(1)}, f32[6,256,1280]{2,1,0:T(8,128)}) fusion(f32[1280]{0:T(1024)} %param.8, f32[6,256]{1,0:T(8,128)S(1)} %add_rsqrt_fusion, f32[6,256]{1,0:T(8,128)S(1)} %broadcast_multiply_fusion.2, bf16[6,256,1280]{2,1,0:T(8,128)(2,1)} %param.6, ...), kind=kOutput, calls=%fused_computation.20 | convolution fusion | flops 396555264 | bytes 13104128 | tf_op jit(solution)/shard_map/bmn,bnd->bmd/dot_general | solution.py:150
  234.3 9.5 %all-to-all-start.5 = ((f32[16,24,128]{2,1,0:T(8,128)}), f32[16,24,128]{2,1,0:T(8,128)S(1)}, u32[]{:S(2)}, u32[]{:S(2)}) async-start(f32[16,24,128]{2,1,0:T(8,128)} %broadcast_in_dim.14), calls=%async_computation.5 | async-start | bytes 393216 | tf_op jit(solution)/shard_map/all_to_all | solution.py:14
  244.4 7.5 %all-to-all-done.5 = f32[16,24,128]{2,1,0:T(8,128)S(1)} async-done(((f32[16,24,128]{2,1,0:T(8,128)}), f32[16,24,128]{2,1,0:T(8,128)S(1)}, u32[]{:S(2)}, u32[]{:S(2)}) %all-to-all-start.5) | async-done | bytes 196640 | tf_op jit(solution)/shard_map/all_to_all | solution.py:14
  252.7 5.7 %all-to-all-start.6 = ((f32[16,24,128]{2,1,0:T(8,128)}), f32[16,24,128]{2,1,0:T(8,128)S(1)}, u32[]{:S(2)}, u32[]{:S(2)}) async-start(f32[16,24,128]{2,1,0:T(8,128)} %broadcast_in_dim.15), calls=%async_computation.6 | async-start | bytes 393216 | tf_op jit(solution)/shard_map/all_to_all | solution.py:14
  258.4 8.5 %fusion.14 = bf16[6,256,1280]{2,1,0:T(8,128)(2,1)} fusion(bf16[6,256,1280]{2,1,0:T(8,128)(2,1)} %param.6, bf16[6,256,1280]{2,1,0:T(8,128)(2,1)} %param.7, f32[6,256,1280]{2,1,0:T(8,128)} %get-tuple-element.19, f32[6,256]{1,0:T(8,128)} %get-tuple-element.20, f32[6,256]{1,0:T(8,128)} %get-tuple-element.21, f32[1280]{0:T(1024)} %param.8, ...), kind=kLoop, calls=%fused_computation.16 | loop fusion | flops 21626880 | bytes 19690496 | tf_op jit(solution)/shard_map/convert_element_type | solution.py:155
  266.8 1.7 all-to-all-done.6
  270.6 8.5 %reduce-scatter.5.cloned.1.call-done = bf16[160,1280]{1,0:T(8,128)(2,1)} async-done(((bf16[1280,1280]{1,0:T(8,128)(2,1)}), bf16[160,1280]{1,0:T(8,128)(2,1)}) %reduce-scatter.5.cloned.1.call-update) | async-done | bytes 409616 | tf_op jit(solution)/shard_map/reduce_scatter | solution.py:120
  (98 shorter events, 45.0 us)
Async XLA Ops:
  7.2 88.0 %copy-start = (bf16[1,1280,1280]{2,1,0:T(8,128)(2,1)S(1)}, bf16[1,1280,1280]{2,1,0:T(8,128)(2,1)}, u32[]{:S(2)}) copy-start(bf16[1,1280,1280]{2,1,0:T(8,128)(2,1)} %param.10) | copy-start | bytes 9830404
  7.2 3.4 %copy-start.1 = (bf16[6,256,1280]{2,1,0:T(8,128)(2,1)S(1)}, bf16[6,256,1280]{2,1,0:T(8,128)(2,1)}, u32[]{:S(2)}) copy-start(bf16[6,256,1280]{2,1,0:T(8,128)(2,1)} %param.6) | copy-start | bytes 11796484
  7.2 4.6 %copy-start.14 = (f32[1280]{0:T(1024)S(1)}, f32[1280]{0:T(1024)}, u32[]{:S(2)}) copy-start(f32[1280]{0:T(1024)} %param.8) | copy-start | bytes 15364
  7.2 4.6 %copy-start.7 = (bf16[1280,32]{0,1:T(8,128)(2,1)S(1)}, bf16[1280,32]{0,1:T(8,128)(2,1)}, u32[]{:S(2)}) copy-start(bf16[1280,32]{0,1:T(8,128)(2,1)} %param.9) | copy-start | bytes 245764
  10.6 214.0 %copy-start.12 = (f32[6,256]{1,0:T(8,128)}, f32[6,256]{1,0:T(8,128)S(1)}, u32[]{:S(2)}) copy-start(f32[6,256]{1,0:T(8,128)S(1)} %broadcast_multiply_fusion.2) | copy-start | bytes 18436
  11.8 212.8 %copy-start.13 = (f32[6,256]{1,0:T(8,128)}, f32[6,256]{1,0:T(8,128)S(1)}, u32[]{:S(2)}) copy-start(f32[6,256]{1,0:T(8,128)S(1)} %add_rsqrt_fusion) | copy-start | bytes 18436
  14.6 0.7 copy-start.5
  15.4 0.6 copy-start.11
  42.5 25.8 %all-to-all-start = ((bf16[16,6,1,2,1280]{4,3,1,2,0:T(2,128)(2,1)}), bf16[16,6,1,2,1280]{4,3,1,2,0:T(2,128)(2,1)}, u32[]{:S(2)}, u32[]{:S(2)}) async-start(bf16[16,6,1,2,1280]{4,3,1,2,0:T(2,128)(2,1)} %constant_dynamic-update-slice_fusion), calls=%async_computation | async-start | bytes 983040 | tf_op jit(solution)/shard_map/all_to_all | solution.py:84
  68.3 19.7 %all-to-all-start.2 = ((bf16[6,16,2,1280]{3,2,0,1:T(2,128)(2,1)}), bf16[6,16,2,1280]{3,2,0,1:T(2,128)(2,1)}, u32[]{:S(2)}, u32[]{:S(2)}) async-start(bf16[6,16,2,1280]{3,2,0,1:T(2,128)(2,1)} %copy.86), calls=%async_computation.2 | async-start | bytes 983040 | tf_op jit(solution)/shard_map/all_to_all | solution.py:97
  72.4 198.1 %reduce-scatter.3.cloned.1.call-start = ((), (), s32[]{:S(2)}) async-start(), calls=%async_computation.9 | async-start | bytes 3686400 | tf_op jit(solution)/shard_map/reduce_scatter | solution.py:121
  74.5 19.6 %collective-permute-start = (bf16[192,1280]{1,0:T(8,128)(2,1)}, bf16[192,1280]{1,0:T(8,128)(2,1)}, u32[]{:S(2)}, u32[]{:S(2)}) collective-permute-start(bf16[192,1280]{1,0:T(8,128)(2,1)} %reshape_reshape.3), channel_id=1, source_target_pairs={{0,1},{1,0},{2,3},{3,2},{4,5},{5,4},{6,7},{7,6},{8,9},{9,8},{10,11... | collective-permute-start | bytes 1474568 | tf_op jit(solution)/shard_map/ppermute | solution.py:20
  90.0 14.1 %collective-permute-start.2 = (bf16[192,1280]{1,0:T(8,128)(2,1)}, bf16[192,1280]{1,0:T(8,128)(2,1)S(1)}, u32[]{:S(2)}, u32[]{:S(2)}) collective-permute-start(bf16[192,1280]{1,0:T(8,128)(2,1)} %reshape.92), channel_id=1, source_target_pairs={{0,1},{1,0},{2,3},{3,2},{4,5},{5,4},{6,7},{7,6},{8,9},{9,8},{10,11... | collective-permute-start | bytes 1474568 | tf_op jit(solution)/shard_map/ppermute | solution.py:20
  95.2 8.9 %copy-start.15 = (bf16[1,1280,1280]{2,1,0:T(8,128)(2,1)S(1)}, bf16[1,1280,1280]{2,1,0:T(8,128)(2,1)}, u32[]{:S(2)}) copy-start(bf16[1,1280,1280]{2,1,0:T(8,128)(2,1)} %param.11) | copy-start | bytes 9830404
  96.7 9.6 %copy-start.17 = (f32[384,1280]{1,0:T(8,128)}, f32[384,1280]{1,0:T(8,128)S(1)}, u32[]{:S(2)}) copy-start(f32[384,1280]{1,0:T(8,128)S(1)} %fusion.22) | copy-start | bytes 5898244
  104.1 2.1 copy-start.9
  106.2 1.0 copy-start.19
  110.9 5.0 %copy-start.16 = (bf16[1,1280,1280]{2,1,0:T(8,128)(2,1)S(1)}, bf16[1,1280,1280]{2,1,0:T(8,128)(2,1)}, u32[]{:S(2)}) copy-start(bf16[1,1280,1280]{2,1,0:T(8,128)(2,1)} %param.11) | copy-start | bytes 9830404
  110.9 5.0 %copy-start.18 = (f32[384,1280]{1,0:T(8,128)S(1)}, f32[384,1280]{1,0:T(8,128)}, u32[]{:S(2)}) copy-start(f32[384,1280]{1,0:T(8,128)} %copy-done.17) | copy-start | bytes 5898244
  113.8 28.7 %collective-permute-start.3 = (bf16[192,1280]{1,0:T(8,128)(2,1)S(1)}, bf16[192,1280]{1,0:T(8,128)(2,1)S(1)}, u32[]{:S(2)}, u32[]{:S(2)}) collective-permute-start(bf16[192,1280]{1,0:T(8,128)(2,1)S(1)} %slice.59), channel_id=1, source_target_pairs={{0,1},{1,0},{2,3},{3,2},{4,5},{5,4},{6,7},{7,6},{8,9},{9,8},{10,11... | collective-permute-start | bytes 1474568 | tf_op jit(solution)/shard_map/ppermute | solution.py:20
  117.7 1.3 copy-start.4
  119.9 54.9 %collective-permute-start.1 = (bf16[192,1280]{1,0:T(8,128)(2,1)}, bf16[192,1280]{1,0:T(8,128)(2,1)}, u32[]{:S(2)}, u32[]{:S(2)}) collective-permute-start(bf16[192,1280]{1,0:T(8,128)(2,1)} %slice.60), channel_id=1, source_target_pairs={{0,1},{1,0},{2,3},{3,2},{4,5},{5,4},{6,7},{7,6},{8,9},{9,8},{10,11... | collective-permute-start | bytes 1474568 | tf_op jit(solution)/shard_map/ppermute | solution.py:20
  145.5 33.5 %all-to-all-start.3 = ((bf16[96,1,2,1280]{3,2,1,0:T(2,128)(2,1)}), bf16[96,1,2,1280]{3,2,1,0:T(2,128)(2,1)}, u32[]{:S(2)}, u32[]{:S(2)}) async-start(bf16[96,1,2,1280]{3,2,1,0:T(2,128)(2,1)} %bitcast.172), calls=%async_computation.3 | async-start | bytes 983040 | tf_op jit(solution)/shard_map/all_to_all | solution.py:108
  153.0 126.0 %reduce-scatter.5.cloned.1.call-start = ((), (), s32[]{:S(2)}) async-start(), calls=%async_computation.10 | async-start | bytes 3686400 | tf_op jit(solution)/shard_map/reduce_scatter | solution.py:120
  178.9 24.6 %all-to-all-start.1 = ((bf16[96,1,2,1280]{3,2,1,0:T(2,128)(2,1)}), bf16[96,1,2,1280]{3,2,1,0:T(2,128)(2,1)}, u32[]{:S(2)}, u32[]{:S(2)}) async-start(bf16[96,1,2,1280]{3,2,1,0:T(2,128)(2,1)} %bitcast.173), calls=%async_computation.1 | async-start | bytes 983040 | tf_op jit(solution)/shard_map/all_to_all | solution.py:108
  203.5 7.8 %copy-start.10 = (f32[6,256,32]{1,2,0:T(8,128)S(1)}, f32[6,256,32]{1,2,0:T(8,128)}, u32[]{:S(2)}) copy-start(f32[6,256,32]{1,2,0:T(8,128)} %get-tuple-element.18) | copy-start | bytes 589828
  207.7 4.0 %copy-start.2 = (bf16[6,256,1280]{2,1,0:T(8,128)(2,1)S(1)}, bf16[6,256,1280]{2,1,0:T(8,128)(2,1)}, u32[]{:S(2)}) copy-start(bf16[6,256,1280]{2,1,0:T(8,128)(2,1)} %param.6) | copy-start | bytes 11796484
  207.7 4.0 %copy-start.3 = (bf16[6,32,1280]{2,1,0:T(8,128)(2,1)S(1)}, bf16[6,32,1280]{2,1,0:T(8,128)(2,1)}, u32[]{:S(2)}) copy-start(bf16[6,32,1280]{2,1,0:T(8,128)(2,1)} %reshape.94) | copy-start | bytes 1474564
  211.7 1.5 copy-start.6
  214.2 1.6 copy-start.20
  214.2 1.6 copy-start.21
  220.3 13.3 %all-to-all-start.4 = ((f32[16,24,128]{2,1,0:T(8,128)}), f32[16,24,128]{2,1,0:T(8,128)S(1)}, u32[]{:S(2)}, u32[]{:S(2)}) async-start(f32[16,24,128]{2,1,0:T(8,128)} %bitcast.175), calls=%async_computation.4 | async-start | bytes 393216 | tf_op jit(solution)/shard_map/all_to_all | solution.py:69
  234.3 17.6 %all-to-all-start.5 = ((f32[16,24,128]{2,1,0:T(8,128)}), f32[16,24,128]{2,1,0:T(8,128)S(1)}, u32[]{:S(2)}, u32[]{:S(2)}) async-start(f32[16,24,128]{2,1,0:T(8,128)} %broadcast_in_dim.14), calls=%async_computation.5 | async-start | bytes 393216 | tf_op jit(solution)/shard_map/all_to_all | solution.py:14
  252.7 15.9 %all-to-all-start.6 = ((f32[16,24,128]{2,1,0:T(8,128)}), f32[16,24,128]{2,1,0:T(8,128)S(1)}, u32[]{:S(2)}, u32[]{:S(2)}) async-start(f32[16,24,128]{2,1,0:T(8,128)} %broadcast_in_dim.15), calls=%async_computation.6 | async-start | bytes 393216 | tf_op jit(solution)/shard_map/all_to_all | solution.py:14
  258.3 10.2 %copy-start.8 = (bf16[1280,32]{0,1:T(8,128)(2,1)S(1)}, bf16[1280,32]{0,1:T(8,128)(2,1)}, u32[]{:S(2)}) copy-start(bf16[1280,32]{0,1:T(8,128)(2,1)} %param.9) | copy-start | bytes 245764
Sparse Core Ops, SparseCore 0:
  111.1 90.7 reduce-scatter.2
  205.0 74.0 reduce-scatter.4
